TPU v7x, 32 devices: a whole 2x2x4 slice. The times are simulated.
32 devices in a mesh: space: 8 (over z, x), tpair: 4 (over y, core).
Axes of the slice: x: 2, y: 2, z: 4, core: 2. Of those that a mesh axis runs over, the one named last changes fastest.
Arguments:
- eigvecs: bfloat16 [4, 2, 3, 64, 1024], P('tpair', None, None, None, 'space'), may hold values from -6 to 6
- momenta: int32 [8, 3], replicated, may hold values from -2 to 2
- perams: bfloat16 [4, 4, 16, 2, 4096], P('tpair'), may hold values from -0.5 to 0.5
- sources: int32 [4], replicated, may hold values from 0 to 3, each once
- spins: int32 [2, 3, 2], replicated, may hold values from 0 to 3
Outputs:
- baryon: float32 [4, 4, 2, 512, 2, 4096], P('tpair', None, None, 'space')
Inputs may be any that keep to these rules, and one draw needn't show every extreme that they name: The entries of sources are distinct.
All inputs are finite; a program needn't handle non-finite values.
Results may differ from a plain program's by a relative error of at most 0.0064.
Values may be sent and summed in bfloat16 or wider, within the bound.
No kernel may reach another device: no remote copies, remote signals or barrier semaphores. Data moves between devices by JAX's collectives and lax.ppermute only.
A program may use at most 128 MiB of HBM per device.

v0:
```python
import jax
import jax.numpy as jnp
import numpy as np
from jax import lax
from jax.sharding import PartitionSpec as P

LEXT = 64


TWO_PI = 6.283185307179586


def pair_tables(vectors):
    upper_rows, upper_cols = np.triu_indices(vectors, 1)
    total_pairs = vectors * vectors // 2
    left_index = np.zeros(total_pairs, np.int32)
    right_index = np.zeros(total_pairs, np.int32)
    left_index[: upper_rows.size] = upper_rows
    right_index[: upper_rows.size] = upper_cols
    position = np.zeros(vectors * vectors, np.int32)
    sign_table = np.zeros(vectors * vectors, np.float32)
    slot_ids = np.arange(upper_rows.size, dtype=np.int32)
    position[upper_rows * vectors + upper_cols] = slot_ids
    sign_table[upper_rows * vectors + upper_cols] = 1.0
    position[upper_cols * vectors + upper_rows] = slot_ids
    sign_table[upper_cols * vectors + upper_rows] = -1.0
    return (left_index, right_index, position, sign_table)


def cross_columns(left_vec, right_vec):
    left_f = left_vec.astype(jnp.float32)
    right_f = right_vec.astype(jnp.float32)
    pieces = []
    for colour in range(3):
        next_one = (colour + 1) % 3
        after_one = (colour + 2) % 3
        real_part = (
            left_f[:, 0, next_one] * right_f[:, 0, after_one]
            - left_f[:, 1, next_one] * right_f[:, 1, after_one]
            - (
                left_f[:, 0, after_one] * right_f[:, 0, next_one]
                - left_f[:, 1, after_one] * right_f[:, 1, next_one]
            )
        )
        imag_part = (
            left_f[:, 0, next_one] * right_f[:, 1, after_one]
            + left_f[:, 1, next_one] * right_f[:, 0, after_one]
            - (
                left_f[:, 0, after_one] * right_f[:, 1, next_one]
                + left_f[:, 1, after_one] * right_f[:, 0, next_one]
            )
        )
        pieces.append(jnp.stack([real_part, imag_part], axis=1).astype(jnp.bfloat16))
    return jnp.stack(pieces, axis=2)


def projected_left(block_vecs, momenta, offset, total_sites):
    site_count = block_vecs.shape[-1]
    site_ids = offset + jnp.arange(site_count, dtype=jnp.int32)
    coords = jnp.stack([site_ids % LEXT, site_ids // LEXT % LEXT, site_ids // (LEXT * LEXT)])
    turns = jnp.mod(jnp.sum(momenta[:, :, None] * coords[None, :, :], axis=1), LEXT)
    angle = turns.astype(jnp.float32) * (TWO_PI / LEXT)
    factor = lax.rsqrt(jnp.float32(24.0 * total_sites))
    cosine = (jnp.cos(angle) * factor)[:, None, None, :]
    sine = (jnp.sin(angle) * factor)[:, None, None, :]
    vfloat = block_vecs.astype(jnp.float32)
    left_real = cosine * vfloat[0][None] + sine * vfloat[1][None]
    left_imag = cosine * vfloat[1][None] - sine * vfloat[0][None]
    upper_half = jnp.stack([left_real, left_imag], axis=0)
    lower_half = jnp.stack([-left_imag, left_real], axis=0)
    stacked = jnp.stack([upper_half, lower_half], axis=0)
    mom_count = momenta.shape[0]
    vectors = block_vecs.shape[2]
    stacked = jnp.transpose(stacked, (0, 3, 5, 1, 2, 4)).reshape(
        6 * site_count, 2 * mom_count * vectors
    )
    return stacked.astype(jnp.bfloat16)


def complex_blocks(blocks):
    tau_real = blocks[..., 0, :, :]
    tau_imag = blocks[..., 1, :, :]
    upper_half = jnp.stack([tau_real, tau_imag], axis=-2)
    lower_half = jnp.stack([-tau_imag, tau_real], axis=-2)
    return jnp.stack([upper_half, lower_half], axis=-4)


def select_blocks(sink_perams, sources, spins, vectors):
    count_times = sink_perams.shape[0]
    pick_time = (sources[:, None] == jnp.arange(count_times, dtype=jnp.int32)[None, :]).astype(
        jnp.bfloat16
    )
    spin_code = spins[:, :, 0] * 4 + spins[:, :, 1]
    pick_spin = (spin_code[:, :, None] == jnp.arange(16, dtype=jnp.int32)).astype(jnp.bfloat16)
    chosen = jnp.einsum(
        "st,cqa,taxy->scqxy", pick_time, pick_spin, sink_perams, preferred_element_type=jnp.float32
    )
    return chosen.astype(jnp.bfloat16).reshape(
        sources.shape[0] * spins.shape[0], 3, 2, vectors, vectors
    )


def on_device(eigvecs, momenta, perams, sources, spins):
    vecs = eigvecs[0]
    vectors = vecs.shape[2]
    sites_here = vecs.shape[3]
    mom_count = momenta.shape[0]
    space_count = lax.axis_size("space")
    offset = lax.axis_index("space") * sites_here
    left_index, right_index, position, sign_table = pair_tables(vectors)
    projected = projected_left(vecs, momenta, offset, sites_here * space_count)
    turned = jnp.transpose(vecs, (2, 0, 1, 3))
    columns = cross_columns(turned[left_index], turned[right_index]).reshape(left_index.size, -1)
    summed = lax.psum_scatter(
        jnp.dot(columns, projected, preferred_element_type=jnp.float32),
        "space",
        scatter_dimension=0,
        tiled=True,
    )
    rounded = summed.astype(jnp.bfloat16).reshape(summed.shape[0], 2, mom_count, vectors)
    arrived = lax.all_to_all(perams, "tpair", split_axis=1, concat_axis=0, tiled=True)
    blocks = select_blocks(arrived[:, 0], sources, spins, vectors)
    ymats = complex_blocks(blocks)
    spread = jnp.einsum(
        "cwmi,swiox->somxc", rounded, ymats[:, 0], preferred_element_type=jnp.float32
    ).astype(jnp.bfloat16)
    count_sc = spread.shape[0]
    spread = spread.reshape(count_sc, 2, mom_count * vectors, summed.shape[0])
    received = lax.all_to_all(spread, "space", split_axis=2, concat_axis=3, tiled=True)
    signs = jnp.asarray(sign_table).astype(jnp.bfloat16)
    whole = received[..., position] * signs
    rows_here = whole.shape[2]
    whole = whole.reshape(count_sc, 2, rows_here, vectors, vectors)
    middle = jnp.einsum(
        "swpjk,swkox->spjox", whole, ymats[:, 2], preferred_element_type=jnp.float32
    ).astype(jnp.bfloat16)
    result = jnp.einsum(
        "spjwk,swjox->spoxk", middle, ymats[:, 1], preferred_element_type=jnp.float32
    )
    return result.reshape(1, sources.shape[0], spins.shape[0], rows_here, 2, vectors * vectors)


def solution(mesh):
    placed = (
        P("tpair", None, None, None, "space"),
        P(),
        P("tpair", None, None, None, None),
        P(),
        P(),
    )
    return jax.shard_map(
        on_device,
        mesh=mesh,
        in_specs=placed,
        out_specs=P("tpair", None, None, "space", None, None),
        check_vma=False,
    )
```

profile of v0, /device:TPU:0, one launch (start us, length us, event | category | flops | bytes accessed | tf_op | source)
XLA Modules:
  0.0 523.4 jit_solution(13831559436044614517)
XLA Ops:
  6.5 0.0 reduce-scatter.2.cloned.1.call-start
  6.6 0.7 broadcast_clamp_fusion.2
  7.3 0.7 broadcast_clamp_fusion.1
  8.0 1.0 bitcast_convert_fusion.2
  9.0 12.4 %gather_fusion.1 = bf16[2048,2,3,128]{3,1,2,0:T(2,128)(2,1)S(1)} fusion(bf16[64,2,3,128]{3,1,2,0:T(2,128)(2,1)S(1)} %get-tuple-element.23, s32[2048]{0:T(1024)S(1)} %broadcast_clamp_fusion.1), kind=kCustom, calls=%fused_computation.1 | custom fusion | bytes 6299648 | tf_op jit(solution)/shard_map/gather | solution.py:113
  21.5 18.8 %gather_fusion = bf16[2048,2,3,128]{3,1,2,0:T(2,128)(2,1)} fusion(bf16[64,2,3,128]{3,1,2,0:T(2,128)(2,1)S(1)} %get-tuple-element.23, s32[2048]{0:T(1024)S(1)} %broadcast_clamp_fusion.2), kind=kCustom, calls=%fused_computation | custom fusion | bytes 6299648 | tf_op jit(solution)/shard_map/gather | solution.py:113
  40.2 4.7 convert_element_type.75
  44.9 2.3 convert_element_type.76
  47.2 8.4 %subtract_convert_fusion.4 = (bf16[2048,1,1,128]{3,1,2,0:T(2,128)(2,1)}, bf16[2048,1,1,128]{3,1,2,0:T(2,128)(2,1)}) fusion(f32[2048,2,3,128]{3,1,2,0:T(2,128)S(1)} %convert_element_type.76, f32[2048,2,3,128]{3,1,2,0:T(2,128)S(1)} %convert_element_type.75), kind=kLoop, calls=%fused_computation.32 | loop fusion | flops 4194304 | bytes 13631488 | tf_op jit(solution)/shard_map/convert.13
  55.7 7.3 %subtract_convert_fusion.1 = (bf16[2048,1,1,128]{3,1,2,0:T(2,128)(2,1)}, bf16[2048,1,1,128]{3,1,2,0:T(2,128)(2,1)}) fusion(f32[2048,2,3,128]{3,1,2,0:T(2,128)S(1)} %convert_element_type.75, f32[2048,2,3,128]{3,1,2,0:T(2,128)S(1)} %convert_element_type.76), kind=kLoop, calls=%fused_computation.29 | loop fusion | flops 4194304 | bytes 9437184 | tf_op jit(solution)/shard_map/convert.8
  63.0 0.0 copy-start.4
  63.0 8.4 %subtract_convert_fusion.5 = (bf16[2048,1,1,128]{3,1,2,0:T(2,128)(2,1)}, bf16[2048,1,1,128]{3,1,2,0:T(2,128)(2,1)}) fusion(f32[2048,2,3,128]{3,1,2,0:T(2,128)S(1)} %convert_element_type.76, f32[2048,2,3,128]{3,1,2,0:T(2,128)S(1)} %convert_element_type.75), kind=kLoop, calls=%fused_computation.33 | loop fusion | flops 4194304 | bytes 13631488 | tf_op jit(solution)/shard_map/convert.12
  71.4 0.0 copy-done.4
  71.4 0.1 multiply_reduce_fusion
  71.5 0.1 cosine_multiply_fusion
  71.5 0.2 fusion.48
  71.7 0.1 copy.84
  71.8 0.1 copy.82
  71.9 0.9 fusion.19
  72.7 1.1 maximum_bitcast_fusion.1
  73.9 1.5 maximum_bitcast_fusion
  75.4 2.6 convert_element_type.80
  77.9 12.2 %maximum_maximum_fusion = bf16[2048,2,3,128]{3,1,2,0:T(2,128)(2,1)S(1)} fusion(bf16[2048,1,1,128]{3,1,2,0:T(2,128)(2,1)} %get-tuple-element.10, bf16[2048,1,1,128]{3,1,2,0:T(2,128)(2,1)} %get-tuple-element.9, bf16[2048,1,1,128]{3,1,2,0:T(2,128)(2,1)} %get-tuple-element.8, bf16[2048,1,1,128]{3,1,2,0:T(2,128)(2,1)} %get-tuple-element.6, ...), kind=kLoop, calls=%fused_computation.15 | loop fusion | flops 18874368 | bytes 6291456 | tf_op jit(solution)/shard_map/stack | solution.py:54
  90.1 6.9 %copy.80 = bf16[2048,2,3,128]{0,3,2,1:T(8,128)(2,1)} copy(bf16[2048,2,3,128]{3,1,2,0:T(2,128)(2,1)S(1)} %maximum_maximum_fusion) | data formatting | bytes 6291456 | tf_op jit(solution)/shard_map/stack | solution.py:54
  97.0 9.2 %fusion.49 = f32[2048,1024]{1,0:T(8,128)} fusion(bf16[2048,768]{0,1:T(8,128)(2,1)} %bitcast.131, bf16[768,1024]{0,1:T(8,128)(2,1)} %convert_element_type.80), kind=kOutput, calls=%fused_computation.88 | convolution fusion | flops 3221225472 | bytes 13107200 | tf_op jit(solution)/shard_map/dot_general | solution.py:115
  106.3 0.0 copy-start.1
  106.3 0.0 copy-start.3
  106.3 0.0 copy-start.5
  106.3 0.0 reduce-scatter.2.cloned.1.call-update
  106.3 1.2 copy-done.1
  107.5 1.6 copy.73
  109.1 4.3 all-to-all-start
  113.3 0.0 copy-done.3
  113.4 14.4 %all-to-all-done = bf16[1,4,16,2,4096]{4,2,3,0,1:T(8,128)(2,1)S(1)} async-done(((bf16[1,4,16,2,4096]{4,2,3,0,1:T(8,128)(2,1)}), bf16[1,4,16,2,4096]{4,2,3,0,1:T(8,128)(2,1)S(1)}, u32[]{:S(2)}, u32[]{:S(2)}) %all-to-all-start) | async-done | bytes 1048608 | tf_op jit(solution)/shard_map/all_to_all | solution.py:121
  127.8 0.4 convolution_bitcast_fusion
  128.2 0.0 copy-done.5
  128.2 0.5 fusion.17
  128.7 0.4 copy.75
  129.1 0.5 reshape.472
  129.6 0.1 fusion.47
  129.7 0.2 copy.112
  129.9 0.2 copy.113
  130.1 0.1 bitcast_negate_fusion
  130.2 0.2 maximum_bitcast_fusion.4
  130.4 126.2 %reduce-scatter.2.cloned.1.call-done = f32[256,1024]{1,0:T(8,128)} async-done(((f32[2048,1024]{1,0:T(8,128)}), f32[256,1024]{1,0:T(8,128)}) %reduce-scatter.2.cloned.1.call-update) | async-done | bytes 1048592 | tf_op jit(solution)/shard_map/reduce_scatter | solution.py:114
  256.7 1.3 convert_element_type.81
  258.0 0.2 copy.86
  258.2 3.3 bitcast_convert_fusion.1
  261.5 8.5 %copy.88 = bf16[8,2,512,256]{3,1,0,2:T(2,128)(2,1)} copy(bf16[8,2,512,256]{3,2,1,0:T(8,128)(2,1)} %bitcast.129) | data formatting | bytes 8388608 | tf_op jit(solution)/shard_map/reshape | solution.py:128
  270.0 0.0 copy-start.2
  270.0 4.9 all-to-all-start.1
  274.9 0.0 copy-done.2
  274.9 92.9 %all-to-all-done.1 = bf16[8,2,512,256]{3,1,0,2:T(2,128)(2,1)} async-done(((bf16[8,2,512,256]{3,1,0,2:T(2,128)(2,1)}), bf16[8,2,512,256]{3,1,0,2:T(2,128)(2,1)}, u32[]{:S(2)}, u32[]{:S(2)}) %all-to-all-start.1) | async-done | bytes 4194336 | tf_op jit(solution)/shard_map/all_to_all | solution.py:129
  367.8 5.7 %copy.89 = bf16[8,2,512,256]{3,2,1,0:T(8,128)(2,1)} copy(bf16[8,2,512,256]{3,1,0,2:T(2,128)(2,1)} %all-to-all-done.1) | data formatting | bytes 8388608 | tf_op jit(solution)/shard_map/all_to_all | solution.py:129
  373.5 9.0 %copy.108 = bf16[8,2,64,8,256]{2,0,4,3,1:T(8,128)(2,1)} copy(bf16[8,2,64,8,256]{4,2,3,1,0:T(8,128)(2,1)} %bitcast.128) | data formatting | bytes 8388608 | tf_op jit(solution)/shard_map/all_to_all | solution.py:129
  382.6 35.5 %gather_fusion.2 = bf16[4096,8,2,64]{3,1,2,0:T(8,128)(2,1)} fusion(bf16[8,2,64,2048]{2,0,3,1:T(8,128)(2,1)} %bitcast.127, s32[4096]{0:T(1024)S(1)} %broadcast_clamp_fusion), kind=kCustom, calls=%fused_computation.2 | custom fusion | bytes 16793600 | tf_op jit(solution)/shard_map/gather | solution.py:131
  418.1 0.0 copy-start
  418.1 22.0 %copy.92 = bf16[8,2,64,64,64]{4,3,1,2,0:T(8,128)(2,1)} copy(bf16[8,2,64,64,64]{2,0,1,4,3:T(8,128)(2,1)} %bitcast.126) | data formatting | bytes 16777216 | tf_op jit(solution)/shard_map/gather | solution.py:131
  440.1 0.0 copy-done
  440.1 19.8 %fusion.10 = f32[8,64,2,64,64]{4,3,1,2,0:T(8,128)} fusion(bf16[8,2,64,64,64]{4,3,1,2,0:T(8,128)(2,1)} %copy.92, bf16[64,64]{1,0:T(8,128)(2,1)S(1)} %copy-done, bf16[8,3,1,64,2,64]{3,5,2,4,0,1:T(8,128)(2,1)S(1)} %get-tuple-element.16, bf16[8,3,1,64,2,64]{3,5,2,4,0,1:T(8,128)(2,1)S(1)} %get-tuple-element.15), kind=kOutput, calls=%fused_computation.9 | convolution fusion | flops 2169503744 | bytes 28327936 | tf_op jit(solution)/shard_map/spjwk,swjox->spoxk/dot_general | solution.py:137
  459.9 27.9 %reshape.476 = f32[1,4,2,64,2,4096]{5,3,4,2,1,0:T(8,128)} reshape(f32[8,64,2,64,64]{4,3,1,2,0:T(8,128)} %fusion.10) | data formatting | bytes 33554432 | tf_op jit(solution)/shard_map/reshape | solution.py:140
  487.8 28.7 %copy.94 = f32[1,4,2,64,2,4096]{5,4,3,2,1,0:T(2,128)} copy(f32[1,4,2,64,2,4096]{5,3,4,2,1,0:T(8,128)} %reshape.476) | data formatting | bytes 33554432 | tf_op jit(solution)/shard_map/reshape | solution.py:140
  (6 shorter events, 0.1 us)
Async XLA Ops:
  6.5 250.1 %reduce-scatter.2.cloned.1.call-start = ((), (), s32[]{:S(2)}) async-start(), calls=%async_computation.3 | async-start | bytes 9437184 | tf_op jit(solution)/shard_map/reduce_scatter | solution.py:114
  63.0 8.4 %copy-start.4 = (s32[8,3]{0,1:T(4,128)S(1)}, s32[8,3]{0,1:T(4,128)}, u32[]{:S(2)}) copy-start(s32[8,3]{0,1:T(4,128)} %param.13) | copy-start | bytes 292
  106.3 1.2 copy-start.1
  106.3 7.1 %copy-start.3 = (s32[2,3,2]{1,2,0:T(2,128)S(1)}, s32[2,3,2]{1,2,0:T(2,128)}, u32[]{:S(2)}) copy-start(s32[2,3,2]{1,2,0:T(2,128)} %param.16) | copy-start | bytes 148
  106.3 21.9 %copy-start.5 = (s32[4]{0:T(128)S(1)}, s32[4]{0:T(128)}, u32[]{:S(2)}) copy-start(s32[4]{0:T(128)} %param.15) | copy-start | bytes 52
  109.1 18.7 %all-to-all-start = ((bf16[1,4,16,2,4096]{4,2,3,0,1:T(8,128)(2,1)}), bf16[1,4,16,2,4096]{4,2,3,0,1:T(8,128)(2,1)S(1)}, u32[]{:S(2)}, u32[]{:S(2)}) async-start(bf16[1,4,16,2,4096]{4,2,3,0,1:T(8,128)(2,1)} %copy.73), calls=%async_computation | async-start | bytes 2097152 | tf_op jit(solution)/shard_map/all_to_all | solution.py:121
  270.0 4.9 copy-start.2
  270.0 97.9 %all-to-all-start.1 = ((bf16[8,2,512,256]{3,1,0,2:T(2,128)(2,1)}), bf16[8,2,512,256]{3,1,0,2:T(2,128)(2,1)}, u32[]{:S(2)}, u32[]{:S(2)}) async-start(bf16[8,2,512,256]{3,1,0,2:T(2,128)(2,1)} %copy.88), calls=%async_computation.2 | async-start | bytes 8388608 | tf_op jit(solution)/shard_map/all_to_all | solution.py:129
  418.1 22.0 %copy-start = (bf16[64,64]{1,0:T(8,128)(2,1)S(1)}, bf16[64,64]{1,0:T(8,128)(2,1)}, u32[]{:S(2)}) copy-start(bf16[64,64]{1,0:T(8,128)(2,1)} %constant.93) | copy-start | bytes 24580
Sparse Core Ops, SparseCore 0:
  106.4 150.1 reduce-scatter.1
where the time goes:
time: 525 us; the launch traced here: 523 us
  waiting for transfers between devices  234 us (45%)
  local copies, waits for them, and re-layouts  183 us (35%)
  other arithmetic  51 us (10%)
  matrix products  33.3 us (6%)
  between operations  13.6 us (3%)
  starting transfers between devices  9.17 us (2%)
    reduce_scatter x1, waiting for transfers between devices, on_device(): lax.psum_scatter(jnp.dot(columns, projected, preferred_element_type=jnp.f...  126 us
    all_to_all x1, waiting for transfers between devices, on_device(): lax.all_to_all(spread, 'space', split_axis=2, concat_axis=3, tiled=True)  92.9 us
    gather x2, local copies, waits for them, and re-layouts, on_device(): whole = received[..., position] * signs  57.5 us
    reshape x2, local copies, waits for them, and re-layouts, on_device(): result.reshape(1, sources.shape[0], spins.shape[0], rows_here, 2, vectors...  56.6 us
    another operation x4, other arithmetic  25 us
    dot_general x1, matrix products, on_device(): jnp.einsum('spjwk,swjox->spoxk', middle, ymats[:, 1], preferred_element_t...  19.8 us
    gather x1, local copies, waits for them, and re-layouts, on_device(): turned[left_index]  18.8 us
    all_to_all x2, local copies, waits for them, and re-layouts, on_device(): lax.all_to_all(spread, 'space', split_axis=2, concat_axis=3, tiled=True)  14.7 us
  transfers between devices with their start and end apart: 3, of which 3 were waited for; matrix products, arithmetic and copies ran while one was open for 1% of the time, Pallas kernels for 0%

commit v1 on v0

v1 whole, which is shorter than its diff:
```python
import functools

import jax
import jax.numpy as jnp
from jax import lax
from jax.experimental import pallas as pl
from jax.experimental.pallas import tpu as pltpu
from jax.sharding import PartitionSpec as P

LEXT = 64
TWO_PI = 6.283185307179586
LANES = 128
NT_DIMS = (((1,), (1,)), ((), ()))
NN_DIMS = (((1,), (0,)), ((), ()))


def phases(momenta, own_momentum, total_sites):
    site_ids = jnp.arange(total_sites, dtype=jnp.int32)
    row = lax.dynamic_index_in_dim(momenta, own_momentum, 0, keepdims=False)
    turns = jnp.mod(
        row[0] * (site_ids % LEXT)
        + row[1] * (site_ids // LEXT % LEXT)
        + row[2] * (site_ids // (LEXT * LEXT)),
        LEXT,
    )
    angle = turns.astype(jnp.float32) * (TWO_PI / LEXT)
    factor = lax.rsqrt(jnp.float32(24.0 * total_sites))
    both = jnp.stack([jnp.cos(angle) * factor, jnp.sin(angle) * factor], axis=0)
    return jnp.transpose(both.reshape(2, total_sites // LANES, LANES), (1, 0, 2))


def elemental_kernel(v_ref, ph_ref, out_ref, vd_ref, p_ref, x_ref, acc_ref, up_ref, low_ref):
    step = pl.program_id(0)
    vectors = v_ref.shape[3]
    half = vectors // 2
    per_chunk = x_ref.shape[0] // vectors

    @pl.when(step == 0)
    def _():
        acc_ref[...] = jnp.zeros_like(acc_ref)

    cosine = ph_ref[0, 0:1, :]
    sine = ph_ref[0, 1:2, :]
    for colour in range(3):
        real = v_ref[0, 0, colour].astype(jnp.float32)
        imag = v_ref[0, 1, colour].astype(jnp.float32)
        for slot, value in enumerate((real, imag, real + imag)):
            vd_ref[3 * slot + colour, 0:vectors, :] = value
            vd_ref[3 * slot + colour, vectors : 2 * vectors, :] = value
        p_real = cosine * real + sine * imag
        p_imag = cosine * imag - sine * real
        rows = (
            (p_real, -p_imag),
            (-p_imag, -p_real),
            (p_imag, p_real),
            (p_real, -p_imag),
        )
        for n, (left, right) in enumerate(rows):
            at = 2 * LANES * colour
            p_ref[n * vectors : (n + 1) * vectors, at : at + LANES] = left.astype(jnp.bfloat16)
            p_ref[n * vectors : (n + 1) * vectors, at + LANES : at + 2 * LANES] = right.astype(
                jnp.bfloat16
            )

    def chunk(index, carry):
        for u in range(per_chunk):
            shift = index * per_chunk + u + 1
            for block in range(vectors // 16):
                a = [vd_ref[n, 16 * block : 16 * block + 16, :] for n in range(9)]
                b = [vd_ref[n, pl.ds(shift + 16 * block, 16), :] for n in range(9)]
                at_row = u * vectors + 16 * block
                for colour in range(3):
                    up = (colour + 1) % 3
                    down = (colour + 2) % 3
                    one = a[up] * b[down] - a[down] * b[up]
                    two = a[3 + up] * b[3 + down] - a[3 + down] * b[3 + up]
                    three = a[6 + up] * b[6 + down] - a[6 + down] * b[6 + up]
                    at = 2 * LANES * colour
                    x_ref[at_row : at_row + 16, at : at + LANES] = (one - two).astype(jnp.bfloat16)
                    x_ref[at_row : at_row + 16, at + LANES : at + 2 * LANES] = (
                        three - (one + two)
                    ).astype(jnp.bfloat16)
        rows = x_ref.shape[0]
        start = pl.multiple_of(index * rows, rows)
        acc_ref[pl.ds(start, rows), :] += lax.dot_general(
            x_ref[...], p_ref[...], NT_DIMS, preferred_element_type=jnp.float32
        )
        return carry

    lax.fori_loop(0, half // per_chunk, chunk, 0)

    @pl.when(step == pl.num_programs(0) - 1)
    def _():
        def spread(index, carry):
            shift = index + 1
            for block in range(vectors // 8):
                start = pl.multiple_of(index * vectors + 8 * block, 8)
                for part in range(2):
                    value = acc_ref[pl.ds(start, 8), part * LANES : (part + 1) * LANES]
                    up_ref[part, pl.ds(8 * block * (2 * vectors + 1) + shift, 8, 2 * vectors + 1), :] = value
                    low_ref[
                        part, pl.ds(8 * block * (vectors + 1) + shift * vectors, 8, vectors + 1), :
                    ] = value
            return carry

        lax.fori_loop(0, half, spread, 0)

        def fold(j, carry):
            k = lax.broadcasted_iota(jnp.int32, (vectors, LANES), 0)
            wide = pl.multiple_of(j * 2 * vectors, vectors)
            narrow = pl.multiple_of(j * vectors, vectors)
            for part in range(2):
                near_up = up_ref[part, pl.ds(wide, vectors), :]
                far_up = up_ref[part, pl.ds(wide + vectors, vectors), :]
                near_low = low_ref[part, pl.ds(narrow, vectors), :]
                far_low = low_ref[part, pl.ds(narrow + vectors * vectors, vectors), :]
                above = jnp.where(k - j <= half, near_up, -far_low)
                below = jnp.where(j - k < half, -near_low, far_up)
                full = jnp.where(k > j, above, jnp.where(k < j, below, 0.0))
                out_ref[part, j] = full.astype(jnp.bfloat16)
            return carry

        lax.fori_loop(0, vectors, fold, 0)


def elementals(gathered, phase):
    owners, _, _, vectors, sites_here = gathered.shape
    per_owner = sites_here // LANES
    steps = owners * per_owner
    half = vectors // 2
    per_chunk = min(8, half)
    return pl.pallas_call(
        elemental_kernel,
        grid=(steps,),
        in_specs=[
            pl.BlockSpec(
                (1, 2, 3, vectors, LANES), lambda s: (s // per_owner, 0, 0, 0, s % per_owner)
            ),
            pl.BlockSpec((1, 2, LANES), lambda s: (s, 0, 0)),
        ],
        out_specs=pl.BlockSpec((2, vectors, vectors, 2 * vectors), lambda s: (0, 0, 0, 0)),
        out_shape=jax.ShapeDtypeStruct((2, vectors, vectors, 2 * vectors), jnp.bfloat16),
        scratch_shapes=[
            pltpu.VMEM((9, 2 * vectors, LANES), jnp.float32),
            pltpu.VMEM((4 * vectors, 6 * LANES), jnp.bfloat16),
            pltpu.VMEM((per_chunk * vectors, 6 * LANES), jnp.bfloat16),
            pltpu.VMEM((half * vectors, 4 * vectors), jnp.float32),
            pltpu.VMEM((2, 2 * vectors * vectors, LANES), jnp.float32),
            pltpu.VMEM((2, 2 * vectors * vectors, LANES), jnp.float32),
        ],
        compiler_params=pltpu.CompilerParams(
            dimension_semantics=("arbitrary",), vmem_limit_bytes=56 << 20
        ),
        cost_estimate=pl.CostEstimate(
            flops=2 * half * vectors * 6 * LANES * 4 * vectors * steps * 8,
            transcendentals=0,
            bytes_accessed=2 * gathered.size + 4 * vectors**3 * 2,
        ),
        name="elementals",
    )(gathered, phase)


def baryon_kernel(e_ref, l0_ref, t1_ref, w2_ref, out_ref, d_ref):
    step = pl.program_id(0)
    vectors = e_ref.shape[1]
    count = l0_ref.shape[0]
    rows_here = count // pl.num_programs(0)
    half = vectors // 2

    @pl.when(step == 0)
    def _():
        left = l0_ref[...]

        def one(j, carry):
            right = jnp.concatenate([e_ref[0, j], e_ref[1, j]], axis=0)
            value = lax.dot_general(left, right, NT_DIMS, preferred_element_type=jnp.float32)
            d_ref[pl.ds(j, count, vectors), :] = value
            return carry

        lax.fori_loop(0, vectors, one, 0, unroll=2)

    lanes = lax.broadcasted_iota(jnp.int32, (vectors, 2 * vectors), 1)
    left1 = t1_ref[0]
    right2 = w2_ref[0]
    group = 8

    def rows(index, carry):
        pieces = []
        for pair in range(group // 2):
            columns = []
            for one in range(2):
                row = (step * rows_here + index * group + 2 * pair + one) * vectors
                plain = d_ref[pl.ds(pl.multiple_of(row, vectors), vectors), :]
                turned = pltpu.roll(plain, vectors, 1)
                turned = jnp.where(lanes < vectors, -turned, turned)
                columns.append(
                    jnp.concatenate(
                        [plain.astype(jnp.bfloat16), turned.astype(jnp.bfloat16)], axis=0
                    )
                )
            right = jnp.concatenate(columns, axis=1)
            middle = lax.dot_general(left1, right, NN_DIMS, preferred_element_type=jnp.float32)
            middle = middle.astype(jnp.bfloat16)
            for one in range(2):
                at = one * 2 * vectors
                part = middle[:, at : at + 2 * vectors]
                pieces.append(jnp.concatenate([part[:half], part[half:]], axis=1))
        stacked = jnp.concatenate(pieces, axis=0)
        value = lax.dot_general(stacked, right2, NN_DIMS, preferred_element_type=jnp.float32)
        base = index * group * half * 2
        for part in range(2):
            out_ref[0, pl.ds(base + part, group * half, 2), :] = value[
                :, part * 2 * vectors : (part + 1) * 2 * vectors
            ]
        return carry

    lax.fori_loop(0, rows_here // group, rows, 0)


def baryons(elemental, l0, t1, w2):
    vectors = elemental.shape[1]
    count_sc = t1.shape[0]
    rows_here = l0.shape[0] // count_sc
    return pl.pallas_call(
        baryon_kernel,
        grid=(count_sc,),
        in_specs=[
            pl.BlockSpec(elemental.shape, lambda s: (0, 0, 0, 0)),
            pl.BlockSpec(l0.shape, lambda s: (0, 0)),
            pl.BlockSpec((1,) + t1.shape[1:], lambda s: (s, 0, 0)),
            pl.BlockSpec((1,) + w2.shape[1:], lambda s: (s, 0, 0)),
        ],
        out_specs=pl.BlockSpec((1, rows_here * vectors, 2 * vectors), lambda s: (s, 0, 0)),
        out_shape=jax.ShapeDtypeStruct(
            (count_sc, rows_here * vectors, 2 * vectors), jnp.float32
        ),
        scratch_shapes=[pltpu.VMEM((l0.shape[0] * vectors, 2 * vectors), jnp.float32)],
        compiler_params=pltpu.CompilerParams(
            dimension_semantics=("arbitrary",), vmem_limit_bytes=56 << 20
        ),
        name="baryons",
    )(elemental, l0, t1, w2)


def chosen_perams(perams, sources, spins):
    count_times = perams.shape[1]
    codes = (spins[:, :, 0] * 4 + spins[:, :, 1]).reshape(-1)
    local = perams[0]
    picked = jnp.stack(
        [
            lax.dynamic_index_in_dim(local, codes[n], 1, keepdims=False)
            for n in range(codes.shape[0])
        ],
        axis=1,
    )
    arrived = lax.all_to_all(picked, "tpair", split_axis=0, concat_axis=0, tiled=True)
    return jnp.stack(
        [
            lax.dynamic_index_in_dim(arrived, sources[s], 0, keepdims=False)
            for s in range(count_times)
        ],
        axis=0,
    )


def on_device(eigvecs, momenta, perams, sources, spins):
    vectors = eigvecs.shape[3]
    sites_here = eigvecs.shape[4]
    mom_count = momenta.shape[0]
    combos = spins.shape[0]
    space_count = lax.axis_size("space")
    place = lax.axis_index("space")
    rows_here = mom_count * vectors // space_count
    count_sc = sources.shape[0] * combos
    own_momentum = place * rows_here // vectors

    tau = chosen_perams(perams, sources, spins)
    tau = tau.reshape(count_sc, 3, 2, vectors, vectors)

    gathered = lax.all_gather(eigvecs[0], "space", axis=0, tiled=False)
    phase = phases(momenta, own_momentum, sites_here * space_count)
    elemental = elementals(gathered, phase)

    flipped = jnp.transpose(tau[:, :2], (0, 1, 4, 2, 3)).reshape(
        count_sc, 2, vectors, 2 * vectors
    )
    l0 = flipped[:, 0]
    if rows_here != vectors:
        l0 = lax.dynamic_slice_in_dim(l0, place * rows_here % vectors, rows_here, 1)
    l0 = l0.reshape(count_sc * rows_here, 2 * vectors)
    t1 = flipped[:, 1].reshape(count_sc, vectors // 2, 2, 2 * vectors)
    t1 = jnp.transpose(t1, (0, 2, 1, 3)).reshape(count_sc, vectors, 2 * vectors)
    real = tau[:, 2, 0]
    imag = tau[:, 2, 1]
    for_real = jnp.concatenate([real, -imag], axis=1)
    for_imag = jnp.concatenate([imag, real], axis=1)
    zero = jnp.zeros_like(for_real)
    w2 = jnp.concatenate(
        [
            jnp.concatenate([for_real, zero, for_imag, zero], axis=2),
            jnp.concatenate([zero, for_real, zero, for_imag], axis=2),
        ],
        axis=1,
    )
    result = baryons(elemental, l0, t1, w2)
    result = result.reshape(count_sc, rows_here, vectors // 2, 2, 2 * vectors)
    result = jnp.transpose(result, (0, 1, 3, 2, 4))
    return result.reshape(1, sources.shape[0], combos, rows_here, 2, vectors * vectors)


def solution(mesh):
    placed = (
        P("tpair", None, None, None, "space"),
        P(),
        P("tpair", None, None, None, None),
        P(),
        P(),
    )
    return jax.shard_map(
        on_device,
        mesh=mesh,
        in_specs=placed,
        out_specs=P("tpair", None, None, "space", None, None),
        check_vma=False,
    )
```

time: 525 us -> 156 us (0.30)
  waiting for transfers between devices: 234 us -> 0.01 us
  local copies, waits for them, and re-layouts: 183 us -> 13.8 us
  Pallas kernels: 0 us -> 76.7 us
  other arithmetic: 51 us -> 6.43 us
  blocking collectives: 0 us -> 34.9 us
  matrix products: 33.3 us -> 0 us
  between operations: 13.6 us -> 19.4 us
    reduce_scatter x1 -> x0, waiting for transfers between devices: 126 us -> none  [on_device(): lax.psum_scatter(jnp.dot(columns, projected, preferred_element_type=jnp.f...]
    all_to_all x2 -> x1, waiting for transfers between devices: 107 us -> 0.01 us  [chosen_perams(): lax.all_to_all(picked, 'tpair', split_axis=0, concat_axis=0, tiled=True)]
    gather x4 -> x0, local copies, waits for them, and re-layouts: 88.7 us -> none  [the longest x2 57.5 us: on_device(): whole = received[..., position] * signs]
    pallas_call x0 -> x2, Pallas kernels: none -> 76.7 us  [the longest x1 46.2 us: baryons(): pl.pallas_call(baryon_kernel, grid=(count_sc,), in_specs=[pl.BlockSpec(el...]
    reshape x4 -> x1, local copies, waits for them, and re-layouts: 65.6 us -> 0.49 us  [on_device(): tau = tau.reshape(count_sc, 3, 2, vectors, vectors)]
    another operation x8 -> x1, other arithmetic: 38.6 us -> 0.71 us  [chosen_perams(): jnp.stack([lax.dynamic_index_in_dim(arrived, sources[s], 0, keepdims=Fals...]
    all_gather x0 -> x1, blocking collectives: none -> 34.9 us  [on_device(): gathered = lax.all_gather(eigvecs[0], 'space', axis=0, tiled=False)]
    dot_general x5 -> x0, matrix products: 33.3 us -> none  [the longest x1 19.8 us: on_device(): jnp.einsum('spjwk,swjox->spoxk', middle, ymats[:, 1], preferred_element_t...]
  transfers between devices with their start and end apart: 3 -> 1, of which waited for: 3 -> 0; matrix products, arithmetic and copies ran while one was open for 1% -> 3% of each run, Pallas kernels for 0% -> 20%
where the time goes in v1:
time: 156 us
  Pallas kernels  76.7 us (49%)
  blocking collectives  34.9 us (22%)
  between operations  19.4 us (12%)
  local copies, waits for them, and re-layouts  13.8 us (9%)
  other arithmetic  6.43 us (4%)
  starting transfers between devices  4.26 us (3%)
    pallas_call x1, Pallas kernels, baryons(): pl.pallas_call(baryon_kernel, grid=(count_sc,), in_specs=[pl.BlockSpec(el...  46.2 us
    all_gather x1, blocking collectives, on_device(): gathered = lax.all_gather(eigvecs[0], 'space', axis=0, tiled=False)  34.9 us
    pallas_call x1, Pallas kernels, elementals(): pl.pallas_call(elemental_kernel, grid=(steps,), in_specs=[pl.BlockSpec((1...  30.5 us
    unnamed x10, local copies, waits for them, and re-layouts  8.36 us
    all_to_all x1, starting transfers between devices, chosen_perams(): lax.all_to_all(picked, 'tpair', split_axis=0, concat_axis=0, tiled=True)  4.26 us
  transfers between devices with their start and end apart: 1, of which 0 were waited for; matrix products, arithmetic and copies ran while one was open for 3% of the time, Pallas kernels for 20%

profile of v1, /device:TPU:0, one launch (start us, length us, event | category | flops | bytes accessed | tf_op | source)
XLA Modules:
  0.0 155.6 jit_solution(9797666999440953513)
XLA Ops:
  0.0 0.0 copy-start
  0.0 0.8 add_reduce_fusion
  0.8 0.1 add.175
  0.9 0.7 fusion.18
  13.1 1.5 bitcast_dynamic-update-slice_fusion.5
  14.6 1.5 bitcast_dynamic-update-slice_fusion.4
  16.1 1.5 bitcast_dynamic-update-slice_fusion.3
  17.6 1.5 bitcast_dynamic-update-slice_fusion.2
  19.1 1.5 bitcast_dynamic-update-slice_fusion.1
  20.6 1.5 bitcast_dynamic-update-slice_fusion
  22.2 4.3 %all-to-all-start = ((bf16[4,6,2,4096]{3,2,1,0:T(2,128)(2,1)}), bf16[4,6,2,4096]{3,2,1,0:T(2,128)(2,1)S(1)}, u32[]{:S(2)}, u32[]{:S(2)}) async-start(bf16[4,6,2,4096]{3,2,1,0:T(2,128)(2,1)} %bitcast_dynamic-update-slice_fusion), calls=%async_computation | async-start | bytes 786432 | tf_op jit(solution)/shard_map/all_to_all | solution.py:256
  26.4 0.0 copy-done
  26.4 0.1 constant_dynamic-slice_fusion.4
  26.5 0.6 fusion.16
  27.1 2.0 %fusion.8 = f32[1,8,128]{2,1,0:T(8,128)S(1)} fusion(s32[]{:T(128)} %bitcast.2, s32[]{:T(128)} %bitcast.1, s32[]{:T(128)} %bitcast), kind=kLoop, calls=%fused_computation.33 | loop fusion | flops 60416 | bytes 4108 | tf_op jit(solution)/shard_map/convert_element_type | solution.py:26
  29.0 0.1 cosine_multiply_fusion
  29.2 34.9 %all_gather.3.v_ref = bf16[8,2,3,64,128]{4,3,2,1,0:T(8,128)(2,1)} all-gather(bf16[1,2,3,64,128]{4,3,2,1,0:T(8,128)(2,1)} %param.5), channel_id=1, replica_groups=mesh['space'=8,'tpair'=4] {'space'}, dimensions={0}, use_global_device_ids=true | all-gather | bytes 884736 | tf_op jit(solution)/shard_map/all_gather | solution.py:280
  64.1 0.6 maximum_bitcast_fusion.ph_ref
  64.7 0.0 copy-start.1
  64.7 30.5 %elementals.1.e_ref = bf16[2,64,64,128]{3,2,1,0:T(8,128)(2,1)} custom-call(bf16[8,2,3,64,128]{4,3,2,1,0:T(8,128)(2,1)} %all_gather.3.v_ref, f32[8,2,128]{2,1,0:T(2,128)} %maximum_bitcast_fusion.ph_ref), custom_call_target="tpu_custom_call" | custom-call | flops 51539607552 | bytes 2883584 | tf_op jit(solution)/shard_map/elementals/pallas_call | solution.py:132
  95.2 0.0 copy-done.1
  95.2 0.7 fusion.17
  103.7 0.0 all-to-all-done
  103.7 0.4 constant_dynamic-slice_fusion.3
  104.1 0.7 pad_maximum_fusion
  104.8 0.5 reshape.245
  105.5 0.2 copy.21
  105.6 0.7 copy.22
  106.3 0.8 copy.27
  107.1 2.2 %maximum_maximum_fusion.w2_ref = bf16[8,256,256]{2,1,0:T(8,128)(2,1)} fusion(bf16[8,64,64]{2,1,0:T(8,128)(2,1)S(1)} %get-tuple-element.6, bf16[8,64,64]{2,1,0:T(8,128)(2,1)S(1)} %get-tuple-element.5, bf16[8,128,64]{2,1,0:T(8,128)(2,1)S(1)} %broadcast_in_dim.3, bf16[8,64,64]{2,1,0:T(8,128)(2,1)S(1)} %fusion.14), kind=kLoop, calls=%fused_computation | loop fusion | flops 12582912 | bytes 1376256 | tf_op jit(solution)/shard_map/concatenate | solution.py:298
  109.3 46.2 %baryons.1 = f32[8,4096,128]{2,1,0:T(8,128)} custom-call(bf16[2,64,64,128]{3,2,1,0:T(8,128)(2,1)} %elementals.1.e_ref, bf16[512,128]{1,0:T(8,128)(2,1)} %bitcast.52, bf16[8,64,128]{2,1,0:T(8,128)(2,1)} %bitcast.53, bf16[8,256,256]{2,1,0:T(8,128)(2,1)} %maximum_maximum_fusion.w2_ref), custom_call_target="tpu_custom_call" | custom-call | tf_op jit(solution)/shard_map/baryons/pallas_call | solution.py:224
  (5 shorter events, 0.2 us)
Async XLA Ops:
  0.0 26.4 %copy-start = (s32[8,3]{0,1:T(4,128)S(1)}, s32[8,3]{0,1:T(4,128)}, u32[]{:S(2)}) copy-start(s32[8,3]{0,1:T(4,128)} %param.6) | copy-start | bytes 292
  22.2 81.5 %all-to-all-start = ((bf16[4,6,2,4096]{3,2,1,0:T(2,128)(2,1)}), bf16[4,6,2,4096]{3,2,1,0:T(2,128)(2,1)S(1)}, u32[]{:S(2)}, u32[]{:S(2)}) async-start(bf16[4,6,2,4096]{3,2,1,0:T(2,128)(2,1)} %bitcast_dynamic-update-slice_fusion), calls=%async_computation | async-start | bytes 786432 | tf_op jit(solution)/shard_map/all_to_all | solution.py:256
  64.7 30.5 %copy-start.1 = (s32[4]{0:T(128)S(1)}, s32[4]{0:T(128)}, u32[]{:S(2)}) copy-start(s32[4]{0:T(128)} %param.8) | copy-start | bytes 52
